TPU v7x, 32 devices: a whole 2x2x4 slice. The times are simulated.
32 devices in a mesh: wide: 8 (over z, y), narrow: 4 (over x, core).
Axes of the slice: x: 2, y: 2, z: 4, core: 2. Of those that a mesh axis runs over, the one named last changes fastest.
Arguments:
- rhs: float32 [3, 32, 32, 128], P(None, 'wide', 'narrow'), may hold values from -12 to 12
- start: float32 [3, 32, 32, 128], P(None, 'wide', 'narrow'), may hold values from -2 to 2
- trans: float32 [3, 32, 32, 128], P(None, 'wide', 'narrow'), may hold values from 0.2 to 2
- accum: float32 [32, 32, 128], P('wide', 'narrow'), may hold values from 2 to 8
- coupling: float32 [3, 3, 32, 32, 128], P(None, None, 'wide', 'narrow'), may hold values from -0.3 to 0.3
- well_cells: int32 [8, 4, 64], P('wide', 'narrow'), may hold values from 0 to 4095
- well_index: float32 [8, 4, 64], P('wide', 'narrow'), may hold values from 1 to 20
- agg_map: int32 [32, 32, 128], P('wide', 'narrow'), may hold values from 0 to 31
- tile_factors: bfloat16 [48, 48, 128, 128], P('wide', 'narrow')
- coarse_inverse: float32 [1024, 1024], P(('wide', 'narrow')), as said below
Outputs:
- iterate: float32 [3, 32, 32, 128], P(None, 'wide', 'narrow')
- residual: float32 [3, 32, 32, 128], P(None, 'wide', 'narrow')
Inputs may be any that keep to these rules, and one draw needn't show every extreme that they name: well_cells names, for each device's 64 connections, one of that device's own 4 * 8 * 128 cells, counted by pair, then column, then position in the tile; connections may share a cell. agg_map names one of the 32 aggregates of the device that owns the cell. coarse_inverse is symmetric.
All inputs are finite; a program needn't handle non-finite values.
Results may differ from a plain program's by a relative error of at most 0.00095.
Values sent between devices are 32-bit elements; how exact they have to be, the bound alone decides.
A program may use at most 64 MiB of HBM per device.

v0:
```python
import jax
import jax.numpy as jnp
from jax import lax
from jax.sharding import PartitionSpec as P

AGG_LOC = 32
SWEEPS = 3
INNER = 3


best_precision = lax.Precision.HIGHEST


def padded(cells, sides, width):
    for axis, dim in sides:
        count = lax.axis_size(axis)
        head = lax.slice_in_dim(cells, 0, width, axis=dim)
        tail = lax.slice_in_dim(cells, cells.shape[dim] - width, cells.shape[dim], axis=dim)
        cells = jnp.concatenate(
            [
                lax.ppermute(tail, axis, [(i, (i + 1) % count) for i in range(count)]),
                cells,
                lax.ppermute(head, axis, [((i + 1) % count, i) for i in range(count)]),
            ],
            axis=dim,
        )
    return cells


def neighbour(values, along, offset):
    along = along % values.ndim
    length = values.shape[along]
    padding = [(0, 0)] * values.ndim
    if offset > 0:
        padding[along] = (0, offset)
        return lax.slice_in_dim(jnp.pad(values, padding), offset, offset + length, axis=along)
    padding[along] = (-offset, 0)
    return lax.slice_in_dim(jnp.pad(values, padding), 0, length, axis=along)


def east_of(values):
    middle = values.shape[-1] // 2
    from_next = neighbour(values, -3, 1)[..., :middle]
    return jnp.concatenate([values[..., middle:], from_next], axis=-1)


def west_of(values):
    middle = values.shape[-1] // 2
    from_prev = neighbour(values, -3, -1)[..., middle:]
    return jnp.concatenate([from_prev, values[..., :middle]], axis=-1)


def prepare(trans, accum_w):
    middle = trans.shape[-1] // 2
    layer_no = lax.broadcasted_iota(jnp.int32, accum_w.shape, accum_w.ndim - 1) % middle
    trans_x = trans[0]
    trans_y = trans[1]
    trans_z = jnp.where(layer_no < middle - 1, trans[2], 0.0)
    face_sum = trans_x + west_of(trans_x) + trans_y + neighbour(trans_y, -2, -1)
    face_sum = face_sum + trans_z + neighbour(trans_z, -1, -1)
    return (trans_x, trans_y, trans_z, accum_w + face_sum)


def operate(values, trans_x, trans_y, trans_z, centre, coupling):
    mixing = jnp.sum(coupling * values[None], axis=1)
    inflow = trans_x * east_of(values) + west_of(trans_x) * west_of(values)
    inflow = inflow + trans_y * neighbour(values, -2, 1)
    inflow = inflow + neighbour(trans_y, -2, -1) * neighbour(values, -2, -1)
    inflow = inflow + trans_z * neighbour(values, -1, 1)
    inflow = inflow + neighbour(trans_z, -1, -1) * neighbour(values, -1, -1)
    return centre * values + mixing - inflow


def tile_apply(values, inverse_diag, factors):
    scaled = (inverse_diag * values).astype(jnp.bfloat16)
    return jnp.einsum("cpyj,pykj->cpyk", scaled, factors, preferred_element_type=jnp.float32)


def local_solve(misfit, coeffs, inverse_diag, factors):
    trans_x, trans_y, trans_z, centre, coupling = coeffs
    update = tile_apply(misfit, inverse_diag, factors)
    for _ in range(INNER - 1):
        applied = operate(update, trans_x, trans_y, trans_z, centre, coupling)
        update = update + tile_apply(misfit - applied, inverse_diag, factors)
    return update


def per_device(
    rhs,
    start,
    trans,
    accum,
    coupling,
    well_cells,
    well_index,
    agg_map,
    tile_factors,
    coarse_inverse,
):
    phases = rhs.shape[0]
    accum_flat = accum.reshape(-1).at[well_cells.reshape(-1)].add(well_index.reshape(-1))
    accum_w = accum_flat.reshape(accum.shape)
    stacked = jnp.concatenate(
        [trans, accum_w[None], coupling.reshape((phases * phases,) + accum.shape)], axis=0
    )
    stacked = jnp.concatenate([stacked, rhs], axis=0)
    rim_wide = padded(stacked, (("wide", 1),), 2)
    rim_full = padded(rim_wide, (("narrow", 2),), 3)
    trans_x, trans_y, trans_z, centre = prepare(rim_full[0:3], rim_full[3])
    coupling_full = rim_full[4:13].reshape((phases, phases) + rim_full.shape[1:])
    full_set = (trans_x, trans_y, trans_z, centre, coupling_full)
    ext_set = tuple((member[..., 1:-1, 1:-1, :] for member in full_set))
    diag_part = jnp.stack([ext_set[4][member, member] for member in range(phases)])
    inverse_diag = 1.0 / (ext_set[3][None] + diag_part)

    def extended_fn(current):
        rim_x = padded(current, (("wide", 1),), 2)
        rim_xy = padded(rim_x, (("narrow", 2),), 3)
        applied = operate(rim_xy, full_set[0], full_set[1], full_set[2], full_set[3], full_set[4])
        extended = (rim_full[13:] - applied)[..., 1:-1, 1:-1, :]
        return (extended, extended[..., 1:-1, 2:-2, :])

    groups = jnp.arange(AGG_LOC, dtype=jnp.int32)
    member_of = (groups[:, None] == agg_map.reshape(1, -1)).astype(jnp.float32)
    current = start
    for _ in range(SWEEPS):
        extended, owned_misfit = extended_fn(current)
        coarse_rhs = jnp.dot(member_of, owned_misfit[0].reshape(-1), precision=best_precision)
        coarse_all = lax.all_gather(coarse_rhs, ("wide", "narrow"), axis=0, tiled=True)
        coarse_sol = jnp.dot(coarse_inverse, coarse_all, precision=best_precision)
        update = local_solve(extended, ext_set, inverse_diag, tile_factors)[..., 1:-1, 2:-2, :]
        lifted = jnp.dot(coarse_sol, member_of, precision=best_precision).reshape(accum.shape)
        current = current + update.at[0].add(lifted)
    final_misfit = extended_fn(current)[1]
    return (current, final_misfit)


def solution(mesh):
    return jax.shard_map(
        per_device,
        mesh=mesh,
        in_specs=(
            P(None, "wide", "narrow", None),
            P(None, "wide", "narrow", None),
            P(None, "wide", "narrow", None),
            P("wide", "narrow", None),
            P(None, None, "wide", "narrow", None),
            P("wide", "narrow", None),
            P("wide", "narrow", None),
            P("wide", "narrow", None),
            P("wide", "narrow", None, None),
            P(("wide", "narrow"), None),
        ),
        out_specs=(P(None, "wide", "narrow", None), P(None, "wide", "narrow", None)),
        check_vma=False,
    )
```

profile of v0, /device:TPU:0, one launch (start us, length us, event | category | flops | bytes accessed | tf_op | source)
XLA Modules:
  0.0 226.2 jit_solution(8377544734950382462)
XLA Ops:
  6.7 3.0 %collective-permute-start = (f32[16,2,8,128]{3,0,2,1:T(8,128)}, f32[16,2,8,128]{3,0,2,1:T(8,128)S(1)}, u32[]{:S(2)}, u32[]{:S(2)}) collective-permute-start(f32[16,2,8,128]{3,0,2,1:T(8,128)} %get-tuple-element.64), channel_id=1, source_target_pairs={{0,4},{4,8},{8,12},{12,16},{16,20},{20,24},{24,28},{28,0},{1,5},{5... | collective-permute-start | bytes 393224 | tf_op jit(solution)/shard_map/ppermute | solution.py:21
  9.7 3.0 %collective-permute-start.1 = (f32[16,2,8,128]{3,0,2,1:T(8,128)S(1)}, f32[16,2,8,128]{3,0,2,1:T(8,128)S(1)}, u32[]{:S(2)}, u32[]{:S(2)}) collective-permute-start(f32[16,2,8,128]{3,0,2,1:T(8,128)S(1)} %get-tuple-element.65), channel_id=1, source_target_pairs={{4,0},{8,4},{12,8},{16,12},{20,16},{24,20},{28,24},{0,28},{5,1},{9... | collective-permute-start | bytes 393224 | tf_op jit(solution)/shard_map/ppermute | solution.py:23
  12.9 4.8 %collective-permute-start.5 = (f32[3,2,8,128]{3,0,2,1:T(4,128)S(1)}, f32[3,2,8,128]{3,0,2,1:T(4,128)S(1)}, u32[]{:S(2)}, u32[]{:S(2)}) collective-permute-start(f32[3,2,8,128]{3,0,2,1:T(4,128)S(1)} %copy.305), channel_id=1, source_target_pairs={{4,0},{8,4},{12,8},{16,12},{20,16},{24,20},{28,24},{0,28},{5,1},{9... | collective-permute-start | bytes 73736 | tf_op jit(solution)/shard_map/ppermute | solution.py:23
  17.6 1.8 collective-permute-done.4
  23.3 1.8 collective-permute-start.2
  25.5 3.1 %collective-permute-done.2 = f32[16,8,3,128]{3,0,2,1:T(8,128)S(1)} collective-permute-done((f32[16,8,3,128]{3,0,2,1:T(8,128)S(1)}, f32[16,8,3,128]{3,0,2,1:T(8,128)S(1)}, u32[]{:S(2)}, u32[]{:S(2)}) %collective-permute-start.2) | collective-permute-done | bytes 196640 | tf_op jit(solution)/shard_map/ppermute | solution.py:21
  38.4 40.3 %all-reduce.66 = f32[1024]{0:T(1024)S(1)} all-reduce(f32[1024]{0:T(1024)S(1)} %dynamic-update-slice.9), channel_id=1, replica_groups=mesh['wide'=8,'narrow'=4] {'wide','narrow'}, use_global_device_ids=true, to_apply=%add.66 | all-reduce | flops 1024 | bytes 8192
  80.1 2.7 %fusion.4 = f32[3,6,12,128]{3,0,2,1:T(4,128)S(1)} fusion(f32[3,6,12,128]{3,0,2,1:T(4,128)S(1)} %fusion.5, bf16[6,12,128,128]{3,2,1,0:T(8,128)(2,1)S(1)} %copy-done, f32[3,6,12,64]{3,0,2,1:T(4,128)} %get-tuple-element.103, f32[3,6,12,64]{3,0,2,1:T(4,128)} %get-tuple-element.104, f32[3,6,12,64]{3,0,2,1:T(4,128)} %get-tuple-element.105, ...), kind=kOutput, calls=%fused_computation.12 | convolution fusion | flops 7741440 | bytes 4104192 | tf_op jit(solution)/shard_map/cpyj,pykj->cpyk/dot_general | solution.py:76
  83.8 2.3 %collective-permute-start.8 = (f32[3,2,8,128]{3,0,2,1:T(4,128)S(1)}, f32[3,2,8,128]{3,0,2,1:T(4,128)S(1)}, u32[]{:S(2)}, u32[]{:S(2)}) collective-permute-start(f32[3,2,8,128]{3,0,2,1:T(4,128)S(1)} %get-tuple-element.122), channel_id=1, source_target_pairs={{0,4},{4,8},{8,12},{12,16},{16,20},{20,24},{24,28},{28,0},{1,5},{5... | collective-permute-start | bytes 73736 | tf_op jit(solution)/shard_map/ppermute | solution.py:21
  86.1 2.5 %collective-permute-start.9 = (f32[3,2,8,128]{3,0,2,1:T(4,128)S(1)}, f32[3,2,8,128]{3,0,2,1:T(4,128)S(1)}, u32[]{:S(2)}, u32[]{:S(2)}) collective-permute-start(f32[3,2,8,128]{3,0,2,1:T(4,128)S(1)} %get-tuple-element.123), channel_id=1, source_target_pairs={{4,0},{8,4},{12,8},{16,12},{20,16},{24,20},{28,24},{0,28},{5,1},{9... | collective-permute-start | bytes 73736 | tf_op jit(solution)/shard_map/ppermute | solution.py:23
  88.5 1.9 collective-permute-done.8
  92.3 1.8 collective-permute-done.10
  98.4 2.2 fusion.3
  102.9 41.2 %all-reduce.67 = f32[1024]{0:T(1024)S(1)} all-reduce(f32[1024]{0:T(1024)S(1)} %dynamic-update-slice.10), channel_id=1, replica_groups=mesh['wide'=8,'narrow'=4] {'wide','narrow'}, use_global_device_ids=true, to_apply=%add.67 | all-reduce | flops 1024 | bytes 8192
  146.2 2.7 %fusion.2 = f32[3,6,12,128]{3,0,2,1:T(4,128)S(1)} fusion(f32[3,6,12,128]{3,0,2,1:T(4,128)S(1)} %fusion.3, bf16[6,12,128,128]{3,2,1,0:T(8,128)(2,1)S(1)} %copy-done, f32[3,6,12,64]{3,0,2,1:T(4,128)} %get-tuple-element.95, f32[3,6,12,64]{3,0,2,1:T(4,128)} %get-tuple-element.96, f32[3,6,12,64]{3,0,2,1:T(4,128)} %get-tuple-element.97, ...), kind=kOutput, calls=%fused_computation.7 | convolution fusion | flops 7741440 | bytes 4104192 | tf_op jit(solution)/shard_map/cpyj,pykj->cpyk/dot_general | solution.py:76
  149.1 2.3 %collective-permute-start.12 = (f32[3,2,8,128]{3,0,2,1:T(4,128)S(1)}, f32[3,2,8,128]{3,0,2,1:T(4,128)S(1)}, u32[]{:S(2)}, u32[]{:S(2)}) collective-permute-start(f32[3,2,8,128]{3,0,2,1:T(4,128)S(1)} %get-tuple-element.120), channel_id=1, source_target_pairs={{0,4},{4,8},{8,12},{12,16},{16,20},{20,24},{24,28},{28,0},{1,5},{5... | collective-permute-start | bytes 73736 | tf_op jit(solution)/shard_map/ppermute | solution.py:21
  151.4 2.5 %collective-permute-start.13 = (f32[3,2,8,128]{3,0,2,1:T(4,128)S(1)}, f32[3,2,8,128]{3,0,2,1:T(4,128)S(1)}, u32[]{:S(2)}, u32[]{:S(2)}) collective-permute-start(f32[3,2,8,128]{3,0,2,1:T(4,128)S(1)} %get-tuple-element.121), channel_id=1, source_target_pairs={{4,0},{8,4},{12,8},{16,12},{20,16},{24,20},{28,24},{0,28},{5,1},{9... | collective-permute-start | bytes 73736 | tf_op jit(solution)/shard_map/ppermute | solution.py:23
  153.9 1.9 collective-permute-done.12
  157.6 1.8 collective-permute-done.14
  167.4 41.2 %all-reduce.68 = f32[1024]{0:T(1024)S(1)} all-reduce(f32[1024]{0:T(1024)S(1)} %dynamic-update-slice.11), channel_id=1, replica_groups=mesh['wide'=8,'narrow'=4] {'wide','narrow'}, use_global_device_ids=true, to_apply=%add.68 | all-reduce | flops 1024 | bytes 8192
  210.0 2.7 %fusion = f32[3,6,12,128]{3,0,2,1:T(4,128)S(1)} fusion(f32[3,6,12,128]{3,0,2,1:T(4,128)S(1)} %fusion.1, bf16[6,12,128,128]{3,2,1,0:T(8,128)(2,1)S(1)} %copy-done, f32[3,6,12,64]{3,0,2,1:T(4,128)} %get-tuple-element.87, f32[3,6,12,64]{3,0,2,1:T(4,128)} %get-tuple-element.88, f32[3,6,12,64]{3,0,2,1:T(4,128)} %get-tuple-element.89, ...), kind=kOutput, calls=%fused_computation.2 | convolution fusion | flops 7741440 | bytes 4104192 | tf_op jit(solution)/shard_map/cpyj,pykj->cpyk/dot_general | solution.py:76
  212.9 2.3 %collective-permute-start.16 = (f32[3,2,8,128]{3,0,2,1:T(4,128)S(1)}, f32[3,2,8,128]{3,0,2,1:T(4,128)S(1)}, u32[]{:S(2)}, u32[]{:S(2)}) collective-permute-start(f32[3,2,8,128]{3,0,2,1:T(4,128)S(1)} %get-tuple-element.118), channel_id=1, source_target_pairs={{0,4},{4,8},{8,12},{12,16},{16,20},{20,24},{24,28},{28,0},{1,5},{5... | collective-permute-start | bytes 73736 | tf_op jit(solution)/shard_map/ppermute | solution.py:21
  215.2 2.5 %collective-permute-start.17 = (f32[3,2,8,128]{3,0,2,1:T(4,128)S(1)}, f32[3,2,8,128]{3,0,2,1:T(4,128)S(1)}, u32[]{:S(2)}, u32[]{:S(2)}) collective-permute-start(f32[3,2,8,128]{3,0,2,1:T(4,128)S(1)} %get-tuple-element.119), channel_id=1, source_target_pairs={{4,0},{8,4},{12,8},{16,12},{20,16},{24,20},{28,24},{0,28},{5,1},{9... | collective-permute-start | bytes 73736 | tf_op jit(solution)/shard_map/ppermute | solution.py:23
  217.7 1.9 collective-permute-done.16
  (245 shorter events, 50.3 us)
Async XLA Ops:
  0.6 31.8 %copy-start = (bf16[6,12,128,128]{3,2,1,0:T(8,128)(2,1)S(1)}, bf16[6,12,128,128]{3,2,1,0:T(8,128)(2,1)}, u32[]{:S(2)}) copy-start(bf16[6,12,128,128]{3,2,1,0:T(8,128)(2,1)} %param.24) | copy-start | bytes 7077892
  6.7 16.5 %collective-permute-start = (f32[16,2,8,128]{3,0,2,1:T(8,128)}, f32[16,2,8,128]{3,0,2,1:T(8,128)S(1)}, u32[]{:S(2)}, u32[]{:S(2)}) collective-permute-start(f32[16,2,8,128]{3,0,2,1:T(8,128)} %get-tuple-element.64), channel_id=1, source_target_pairs={{0,4},{4,8},{8,12},{12,16},{16,20},{20,24},{24,28},{28,0},{1,5},{5... | collective-permute-start | bytes 393224 | tf_op jit(solution)/shard_map/ppermute | solution.py:21
  9.7 13.5 %collective-permute-start.1 = (f32[16,2,8,128]{3,0,2,1:T(8,128)S(1)}, f32[16,2,8,128]{3,0,2,1:T(8,128)S(1)}, u32[]{:S(2)}, u32[]{:S(2)}) collective-permute-start(f32[16,2,8,128]{3,0,2,1:T(8,128)S(1)} %get-tuple-element.65), channel_id=1, source_target_pairs={{4,0},{8,4},{12,8},{16,12},{20,16},{24,20},{28,24},{0,28},{5,1},{9... | collective-permute-start | bytes 393224 | tf_op jit(solution)/shard_map/ppermute | solution.py:23
  12.8 6.7 %collective-permute-start.4 = (f32[3,2,8,128]{3,0,2,1:T(4,128)S(1)}, f32[3,2,8,128]{3,0,2,1:T(4,128)S(1)}, u32[]{:S(2)}, u32[]{:S(2)}) collective-permute-start(f32[3,2,8,128]{3,0,2,1:T(4,128)S(1)} %copy.304), channel_id=1, source_target_pairs={{0,4},{4,8},{8,12},{12,16},{16,20},{20,24},{24,28},{28,0},{1,5},{5... | collective-permute-start | bytes 73736 | tf_op jit(solution)/shard_map/ppermute | solution.py:21
  12.9 6.6 %collective-permute-start.5 = (f32[3,2,8,128]{3,0,2,1:T(4,128)S(1)}, f32[3,2,8,128]{3,0,2,1:T(4,128)S(1)}, u32[]{:S(2)}, u32[]{:S(2)}) collective-permute-start(f32[3,2,8,128]{3,0,2,1:T(4,128)S(1)} %copy.305), channel_id=1, source_target_pairs={{4,0},{8,4},{12,8},{16,12},{20,16},{24,20},{28,24},{0,28},{5,1},{9... | collective-permute-start | bytes 73736 | tf_op jit(solution)/shard_map/ppermute | solution.py:23
  19.5 3.6 %collective-permute-start.6 = (f32[3,8,3,128]{3,0,2,1:T(4,128)S(1)}, f32[3,8,3,128]{3,0,2,1:T(4,128)S(1)}, u32[]{:S(2)}, u32[]{:S(2)}) collective-permute-start(f32[3,8,3,128]{3,0,2,1:T(4,128)S(1)} %get-tuple-element.116), channel_id=1, source_target_pairs={{0,1},{1,2},{2,3},{3,0},{4,5},{5,6},{6,7},{7,4},{8,9},{9,10},{10,1... | collective-permute-start | bytes 110600 | tf_op jit(solution)/shard_map/ppermute | solution.py:21
  19.6 3.5 %collective-permute-start.7 = (f32[3,8,3,128]{3,0,2,1:T(4,128)S(1)}, f32[3,8,3,128]{3,0,2,1:T(4,128)S(1)}, u32[]{:S(2)}, u32[]{:S(2)}) collective-permute-start(f32[3,8,3,128]{3,0,2,1:T(4,128)S(1)} %get-tuple-element.117), channel_id=1, source_target_pairs={{1,0},{2,1},{3,2},{0,3},{5,4},{6,5},{7,6},{4,7},{9,8},{10,9},{11,1... | collective-permute-start | bytes 110600 | tf_op jit(solution)/shard_map/ppermute | solution.py:23
  23.3 5.2 %collective-permute-start.2 = (f32[16,8,3,128]{3,0,2,1:T(8,128)S(1)}, f32[16,8,3,128]{3,0,2,1:T(8,128)S(1)}, u32[]{:S(2)}, u32[]{:S(2)}) collective-permute-start(f32[16,8,3,128]{3,0,2,1:T(8,128)S(1)} %get-tuple-element.59), channel_id=1, source_target_pairs={{0,1},{1,2},{2,3},{3,0},{4,5},{5,6},{6,7},{7,4},{8,9},{9,10},{10,1... | collective-permute-start | bytes 589832 | tf_op jit(solution)/shard_map/ppermute | solution.py:21
  25.1 4.6 %collective-permute-start.3 = (f32[16,8,3,128]{3,0,2,1:T(8,128)S(1)}, f32[16,8,3,128]{3,0,2,1:T(8,128)S(1)}, u32[]{:S(2)}, u32[]{:S(2)}) collective-permute-start(f32[16,8,3,128]{3,0,2,1:T(8,128)S(1)} %get-tuple-element.60), channel_id=1, source_target_pairs={{1,0},{2,1},{3,2},{0,3},{5,4},{6,5},{7,6},{4,7},{9,8},{10,9},{11,1... | collective-permute-start | bytes 589832 | tf_op jit(solution)/shard_map/ppermute | solution.py:23
  30.5 64.3 %copy-start.2 = (f32[8,14,128]{2,1,0:T(8,128)}, f32[8,14,128]{2,1,0:T(8,128)S(1)}, u32[]{:S(2)}) copy-start(f32[8,14,128]{2,1,0:T(8,128)S(1)} %get-tuple-element.130) | copy-start | bytes 172036
  30.9 65.6 %copy-start.4 = (f32[6,12,128]{2,1,0:T(8,128)}, f32[6,12,128]{2,1,0:T(8,128)S(1)}, u32[]{:S(2)}) copy-start(f32[6,12,128]{2,1,0:T(8,128)S(1)} %copy.186) | copy-start | bytes 110596
  83.8 6.7 %collective-permute-start.8 = (f32[3,2,8,128]{3,0,2,1:T(4,128)S(1)}, f32[3,2,8,128]{3,0,2,1:T(4,128)S(1)}, u32[]{:S(2)}, u32[]{:S(2)}) collective-permute-start(f32[3,2,8,128]{3,0,2,1:T(4,128)S(1)} %get-tuple-element.122), channel_id=1, source_target_pairs={{0,4},{4,8},{8,12},{12,16},{16,20},{20,24},{24,28},{28,0},{1,5},{5... | collective-permute-start | bytes 73736 | tf_op jit(solution)/shard_map/ppermute | solution.py:21
  86.1 4.3 %collective-permute-start.9 = (f32[3,2,8,128]{3,0,2,1:T(4,128)S(1)}, f32[3,2,8,128]{3,0,2,1:T(4,128)S(1)}, u32[]{:S(2)}, u32[]{:S(2)}) collective-permute-start(f32[3,2,8,128]{3,0,2,1:T(4,128)S(1)} %get-tuple-element.123), channel_id=1, source_target_pairs={{4,0},{8,4},{12,8},{16,12},{20,16},{24,20},{28,24},{0,28},{5,1},{9... | collective-permute-start | bytes 73736 | tf_op jit(solution)/shard_map/ppermute | solution.py:23
  90.5 3.6 %collective-permute-start.10 = (f32[3,8,3,128]{3,0,2,1:T(4,128)S(1)}, f32[3,8,3,128]{3,0,2,1:T(4,128)S(1)}, u32[]{:S(2)}, u32[]{:S(2)}) collective-permute-start(f32[3,8,3,128]{3,0,2,1:T(4,128)S(1)} %get-tuple-element.114), channel_id=1, source_target_pairs={{0,1},{1,2},{2,3},{3,0},{4,5},{5,6},{6,7},{7,4},{8,9},{9,10},{10,1... | collective-permute-start | bytes 110600 | tf_op jit(solution)/shard_map/ppermute | solution.py:21
  90.5 3.8 %collective-permute-start.11 = (f32[3,8,3,128]{3,0,2,1:T(4,128)S(1)}, f32[3,8,3,128]{3,0,2,1:T(4,128)S(1)}, u32[]{:S(2)}, u32[]{:S(2)}) collective-permute-start(f32[3,8,3,128]{3,0,2,1:T(4,128)S(1)} %get-tuple-element.115), channel_id=1, source_target_pairs={{1,0},{2,1},{3,2},{0,3},{5,4},{6,5},{7,6},{4,7},{9,8},{10,9},{11,1... | collective-permute-start | bytes 110600 | tf_op jit(solution)/shard_map/ppermute | solution.py:23
  100.6 45.7 %copy-start.5 = (f32[6,12,128]{2,1,0:T(8,128)S(1)}, f32[6,12,128]{2,1,0:T(8,128)}, u32[]{:S(2)}) copy-start(f32[6,12,128]{2,1,0:T(8,128)} %copy-done.4) | copy-start | bytes 110596
  149.1 6.7 %collective-permute-start.12 = (f32[3,2,8,128]{3,0,2,1:T(4,128)S(1)}, f32[3,2,8,128]{3,0,2,1:T(4,128)S(1)}, u32[]{:S(2)}, u32[]{:S(2)}) collective-permute-start(f32[3,2,8,128]{3,0,2,1:T(4,128)S(1)} %get-tuple-element.120), channel_id=1, source_target_pairs={{0,4},{4,8},{8,12},{12,16},{16,20},{20,24},{24,28},{28,0},{1,5},{5... | collective-permute-start | bytes 73736 | tf_op jit(solution)/shard_map/ppermute | solution.py:21
  151.4 4.3 %collective-permute-start.13 = (f32[3,2,8,128]{3,0,2,1:T(4,128)S(1)}, f32[3,2,8,128]{3,0,2,1:T(4,128)S(1)}, u32[]{:S(2)}, u32[]{:S(2)}) collective-permute-start(f32[3,2,8,128]{3,0,2,1:T(4,128)S(1)} %get-tuple-element.121), channel_id=1, source_target_pairs={{4,0},{8,4},{12,8},{16,12},{20,16},{24,20},{28,24},{0,28},{5,1},{9... | collective-permute-start | bytes 73736 | tf_op jit(solution)/shard_map/ppermute | solution.py:23
  155.8 3.6 %collective-permute-start.14 = (f32[3,8,3,128]{3,0,2,1:T(4,128)S(1)}, f32[3,8,3,128]{3,0,2,1:T(4,128)S(1)}, u32[]{:S(2)}, u32[]{:S(2)}) collective-permute-start(f32[3,8,3,128]{3,0,2,1:T(4,128)S(1)} %get-tuple-element.112), channel_id=1, source_target_pairs={{0,1},{1,2},{2,3},{3,0},{4,5},{5,6},{6,7},{7,4},{8,9},{9,10},{10,1... | collective-permute-start | bytes 110600 | tf_op jit(solution)/shard_map/ppermute | solution.py:21
  155.9 3.8 %collective-permute-start.15 = (f32[3,8,3,128]{3,0,2,1:T(4,128)S(1)}, f32[3,8,3,128]{3,0,2,1:T(4,128)S(1)}, u32[]{:S(2)}, u32[]{:S(2)}) collective-permute-start(f32[3,8,3,128]{3,0,2,1:T(4,128)S(1)} %get-tuple-element.113), channel_id=1, source_target_pairs={{1,0},{2,1},{3,2},{0,3},{5,4},{6,5},{7,6},{4,7},{9,8},{10,9},{11,1... | collective-permute-start | bytes 110600 | tf_op jit(solution)/shard_map/ppermute | solution.py:23
  212.9 6.7 %collective-permute-start.16 = (f32[3,2,8,128]{3,0,2,1:T(4,128)S(1)}, f32[3,2,8,128]{3,0,2,1:T(4,128)S(1)}, u32[]{:S(2)}, u32[]{:S(2)}) collective-permute-start(f32[3,2,8,128]{3,0,2,1:T(4,128)S(1)} %get-tuple-element.118), channel_id=1, source_target_pairs={{0,4},{4,8},{8,12},{12,16},{16,20},{20,24},{24,28},{28,0},{1,5},{5... | collective-permute-start | bytes 73736 | tf_op jit(solution)/shard_map/ppermute | solution.py:21
  215.2 4.3 %collective-permute-start.17 = (f32[3,2,8,128]{3,0,2,1:T(4,128)S(1)}, f32[3,2,8,128]{3,0,2,1:T(4,128)S(1)}, u32[]{:S(2)}, u32[]{:S(2)}) collective-permute-start(f32[3,2,8,128]{3,0,2,1:T(4,128)S(1)} %get-tuple-element.119), channel_id=1, source_target_pairs={{4,0},{8,4},{12,8},{16,12},{20,16},{24,20},{28,24},{0,28},{5,1},{9... | collective-permute-start | bytes 73736 | tf_op jit(solution)/shard_map/ppermute | solution.py:23
  219.6 3.6 %collective-permute-start.18 = (f32[3,8,3,128]{3,0,2,1:T(4,128)S(1)}, f32[3,8,3,128]{3,0,2,1:T(4,128)S(1)}, u32[]{:S(2)}, u32[]{:S(2)}) collective-permute-start(f32[3,8,3,128]{3,0,2,1:T(4,128)S(1)} %get-tuple-element.110), channel_id=1, source_target_pairs={{0,1},{1,2},{2,3},{3,0},{4,5},{5,6},{6,7},{7,4},{8,9},{9,10},{10,1... | collective-permute-start | bytes 110600 | tf_op jit(solution)/shard_map/ppermute | solution.py:21
  219.7 3.8 %collective-permute-start.19 = (f32[3,8,3,128]{3,0,2,1:T(4,128)S(1)}, f32[3,8,3,128]{3,0,2,1:T(4,128)S(1)}, u32[]{:S(2)}, u32[]{:S(2)}) collective-permute-start(f32[3,8,3,128]{3,0,2,1:T(4,128)S(1)} %get-tuple-element.111), channel_id=1, source_target_pairs={{1,0},{2,1},{3,2},{0,3},{5,4},{6,5},{7,6},{4,7},{9,8},{10,9},{11,1... | collective-permute-start | bytes 110600 | tf_op jit(solution)/shard_map/ppermute | solution.py:23
  (37 other events, 104.7 us)
where the time goes:
time: 229 us; the launch traced here: 226 us
  blocking collectives  123 us (54%)
  starting transfers between devices  34.2 us (15%)
  matrix products  22.9 us (10%)
  waiting for transfers between devices  18.4 us (8%)
  local copies, waits for them, and re-layouts  13.6 us (6%)
  other arithmetic  12.5 us (5%)
    unnamed x3, blocking collectives  123 us
    ppermute x10, starting transfers between devices, padded(): lax.ppermute(head, axis, [((i + 1) % count, i) for i in range(count)])  22.1 us
    dot_general x9, matrix products, tile_apply(): jnp.einsum('cpyj,pykj->cpyk', scaled, factors, preferred_element_type=jnp...  17 us
    ppermute x10, waiting for transfers between devices, padded(): lax.ppermute(tail, axis, [(i, (i + 1) % count) for i in range(count)])  16.2 us
    ppermute x10, starting transfers between devices, padded(): lax.ppermute(tail, axis, [(i, (i + 1) % count) for i in range(count)])  12.1 us
    unnamed x98, local copies, waits for them, and re-layouts  4.69 us
  transfers between devices with their start and end apart: 20, of which 13 were waited for; matrix products, arithmetic and copies ran while one was open for 1% of the time, Pallas kernels for 0%

commit v1 on v0

v1 whole, which is shorter than its diff:
```python
import functools

import jax
import jax.numpy as jnp
from jax import lax
from jax.experimental import pallas as pl
from jax.experimental.pallas import tpu as pltpu
from jax.sharding import PartitionSpec as P

SWEEPS = 3
HIGHEST = lax.Precision.HIGHEST
NT = (((1,), (1,)), ((), ()))
F32 = jnp.float32

DIRS = ((-1, 0), (1, 0), (0, -1), (0, 1), (-1, -1), (-1, 1), (1, -1), (1, 1))


def halo_pieces(px, cy, depth_x, depth_y):
    pieces = []
    for dx, dy in DIRS:
        if dx == 0:
            sp, dp, np_ = 2, 2, px
        elif dx > 0:
            sp, dp, np_ = 2 + px - depth_x, 2 - depth_x, depth_x
        else:
            sp, dp, np_ = 2, 2 + px, depth_x
        if dy == 0:
            sr, dr, nr = 0, 0, cy
        elif dy > 0:
            sr, dr, nr = cy - depth_y, 2 * cy - depth_y, depth_y
        else:
            sr, dr, nr = 0, cy, depth_y
        pieces.append(((sp, sr), (dp, dr), (np_, nr)))
    return pieces


def body(
    nw, nn,
    rhs, start, trans, accum, coupling, cells, widx, agg, tiles, cinv,
    out_it, out_res,
    COEF, CUR, W1, W2, H, DER, TF, CI, AG, ACC, GN, GW, XN, XW,
    loc, hs, hr, cs, cr, ns, nr, ws, wr,
):
    phases = rhs.shape[0]
    px, cy, tile = accum.shape
    box = px + 2
    half = tile // 2
    aggs = CI.shape[0]
    me_w, me_n = lax.axis_index("wide"), lax.axis_index("narrow")

    def dev(dw, dn):
        return {"wide": lax.rem(me_w + dw + nw, nw), "narrow": lax.rem(me_n + dn + nn, nn)}

    own = pl.ds(2, px)
    top = pl.ds(0, cy)
    nch = COEF.shape[0]
    first_rhs = nch - phases
    copies = [
        (accum, ACC),
        (trans, COEF.at[pl.ds(0, 3), own, top]),
        (start, CUR.at[0, :, own, top]),
        (coupling, COEF.at[pl.ds(4, phases * phases), own, top]),
        (rhs, COEF.at[pl.ds(first_rhs, phases), own, top]),
        (agg, AG),
        (cinv, CI),
        (tiles, TF),
    ]
    local = [pltpu.make_async_copy(s, d, loc.at[k]) for k, (s, d) in enumerate(copies)]
    for c in local:
        c.start()

    barrier = pltpu.get_barrier_semaphore()
    peers = [(0, d) for d in range(1, nn)] + [(d, 0) for d in range(1, nw)]
    peers += [d for d in DIRS if d[0] and d[1]]
    for d in peers:
        pl.semaphore_signal(barrier, inc=1, device_id=dev(*d), device_id_type=pl.DeviceIdType.MESH)

    conn = cells.shape[-1]
    cell_row = cells[...]
    rows_own = px * cy
    hit_r = lax.broadcasted_iota(jnp.int32, (rows_own, conn), 0) == cell_row // tile
    hit_l = lax.broadcasted_iota(jnp.int32, (tile, conn), 0) == cell_row % tile
    left = jnp.where(hit_r, jnp.broadcast_to(widx[...], (rows_own, conn)), 0.0)
    right = jnp.where(hit_l, 1.0, 0.0)
    wells = lax.dot_general(left, right, NT, precision=HIGHEST, preferred_element_type=F32)
    local[0].wait()
    COEF[3, 2 : 2 + px, 0:cy, :] = ACC[...] + wells.reshape(px, cy, tile)
    for c in local[1:5]:
        c.wait()
    pl.semaphore_wait(barrier, len(peers))

    def remote(src, dst, ss, rs, d):
        return pltpu.make_async_remote_copy(
            src_ref=src, dst_ref=dst, send_sem=ss, recv_sem=rs,
            device_id=dev(*d), device_id_type=pl.DeviceIdType.MESH,
        )

    pieces = halo_pieces(px, cy, 2, 3)

    def halo(e):
        out = []
        for k, d in enumerate(DIRS):
            (sp, sr), (dp, dr), (npair, nrow) = pieces[k]
            out.append(remote(
                CUR.at[e, :, pl.ds(sp, npair), pl.ds(sr, nrow)],
                CUR.at[e, :, pl.ds(dp, npair), pl.ds(dr, nrow)],
                hs.at[e, k], hr.at[e, k], d))
        return out

    coef = []
    for k, d in enumerate(DIRS):
        (sp, sr), (dp, dr), (npair, nrow) = halo_pieces(px, cy, 1, 3)[k]
        coef.append(remote(
            COEF.at[:, pl.ds(sp, npair), pl.ds(sr, nrow)],
            COEF.at[:, pl.ds(dp, npair), pl.ds(dr, nrow)],
            cs.at[k], cr.at[k], d))
    extra = len(DIRS)
    for k, d in enumerate(DIRS):
        if d[0] > 0:
            (sp, sr), (dp, dr), (npair, nrow) = pieces[k]
            coef.append(remote(
                COEF.at[pl.ds(0, 1), pl.ds(sp, 1), pl.ds(sr, nrow)],
                COEF.at[pl.ds(0, 1), pl.ds(dp, 1), pl.ds(dr, nrow)],
                cs.at[extra], cr.at[extra], d))
            extra += 1
    for c in halo(0) + coef:
        c.start()

    lane = lax.broadcasted_iota(jnp.int32, (2 * cy, tile), 1)
    low = lane < half
    roll = pltpu.roll

    zero16 = jnp.zeros((2 * cy, tile), F32)
    for c in range(phases):
        for w in (W1, W2):
            w[c, 0] = zero16
            w[c, box + 1] = zero16
        W2[c, 1] = zero16
        W2[c, box] = zero16
    for c in local[5:]:
        c.wait()
    for c in coef:
        c.wait_recv()

    for b in range(box):
        tx = COEF[0, b + 1]
        txw = jnp.where(low, roll(COEF[0, b], half, 1), roll(tx, half, 1))
        ty = COEF[1, b + 1]
        tys = roll(ty, 1, 0)
        tz = jnp.where(lane % half < half - 1, COEF[2, b + 1], 0.0)
        tzd = roll(tz, 1, 1)
        centre = COEF[3, b + 1] + (tx + txw + ty + tys + tz + tzd)
        DER[0, b] = txw
        DER[1, b] = tys
        DER[2, b] = tz
        DER[3, b] = tzd
        for c in range(phases):
            diag = centre + COEF[4 + c * phases + c, b + 1]
            DER[4 + c, b] = diag
            DER[4 + phases + c, b] = 1.0 / diag

    def operate(read, boxes):
        swapped = {}

        def swap(c, idx):
            if (c, idx) not in swapped:
                swapped[c, idx] = roll(read(c, idx), half, 1)
            return swapped[c, idx]

        for b in boxes:
            values = [read(c, b + 1) for c in range(phases)]
            result = []
            for c in range(phases):
                v = values[c]
                east = jnp.where(low, swap(c, b + 1), swap(c, b + 2))
                west = jnp.where(low, swap(c, b), swap(c, b + 1))
                total = DER[4 + c, b] * v
                for o in range(phases):
                    if o != c:
                        total = total + COEF[4 + c * phases + o, b + 1] * values[o]
                inflow = COEF[0, b + 1] * east + DER[0, b] * west
                inflow = inflow + COEF[1, b + 1] * roll(v, 2 * cy - 1, 0)
                inflow = inflow + DER[1, b] * roll(v, 1, 0)
                inflow = inflow + DER[2, b] * roll(v, tile - 1, 1)
                inflow = inflow + DER[3, b] * roll(v, 1, 1)
                result.append(total - inflow)
            yield b, result

    row = lax.broadcasted_iota(jnp.int32, (phases * cy, tile), 0) % cy

    def product(b, q, chosen):
        stack = jnp.concatenate(q, axis=0)
        lhs = jnp.concatenate(
            [jnp.where(row == r, stack, 0.0) for r, _ in chosen], axis=1).astype(jnp.bfloat16)
        factors = jnp.concatenate([TF[b, t] for _, t in chosen], axis=1)
        out = lax.dot_general(lhs, factors, NT, preferred_element_type=F32)
        return [out[c * cy : (c + 1) * cy] for c in range(phases)]

    ring_a = tuple((y, y + 2) for y in range(cy))
    ring_b = ((0, cy + 2), (1, cy + 3), (cy - 2, 0), (cy - 1, 1))
    near_b = ((0, cy + 2), (cy - 1, 1))
    inner = range(1, box - 1)

    def scaled(b, h):
        return [DER[4 + phases + c, b] * h[c] for c in range(phases)]

    agg_iota = lax.broadcasted_iota(jnp.int32, (aggs, tile), 0)
    lane8 = lax.broadcasted_iota(jnp.int32, (cy, tile), 1)
    ones = jnp.ones((cy, tile), F32)

    def sweep(s, carry):
        for c in halo(s):
            c.wait_recv()
        acc = jnp.zeros((aggs, tile), F32)
        for b, applied in operate(lambda c, idx: CUR[s, c, idx], range(box)):
            h = [COEF[first_rhs + c, b + 1] - applied[c] for c in range(phases)]
            for c in range(phases):
                H[c, b] = h[c]
            if b in inner:
                for y in range(cy):
                    ids = AG[pl.ds((b - 1) * cy + y, 1), :]
                    acc = acc + jnp.where(agg_iota == ids, h[0][y : y + 1], 0.0)
        wide_acc = jnp.concatenate([acc] * (tile // aggs), axis=0)
        XN[s] = lax.dot_general(ones, wide_acc, NT, precision=HIGHEST, preferred_element_type=F32)
        near = [remote(XN.at[s], GN.at[s, d - 1], ns.at[s, d - 1], nr.at[s, d - 1], (0, d))
                for d in range(1, nn)]
        for c in near:
            c.start()

        for b in range(box):
            q = scaled(b, [H[c, b] for c in range(phases)])
            upper = product(b, [v[:cy] for v in q], ring_a)
            lower = product(b, [v[cy:] for v in q], ring_b if b in inner else near_b)
            for c in range(phases):
                W1[c, b + 1, 0:cy] = upper[c]
                W1[c, b + 1, cy : 2 * cy] = lower[c]

        for c in near:
            c.wait_recv()
        owner = lane8 // aggs
        line = XN[s]
        for d in range(1, nn):
            line = jnp.where(owner == lax.rem(me_n - d + nn, nn), GN[s, d - 1], line)
        XW[s] = line
        far = [remote(XW.at[s], GW.at[s, d - 1], ws.at[s, d - 1], wr.at[s, d - 1], (d, 0))
               for d in range(1, nw)]
        for c in far:
            c.start()

        for b, applied in operate(lambda c, idx: W1[c, idx], range(box)):
            q = scaled(b, [H[c, b] - applied[c] for c in range(phases)])
            upper = product(b, [v[:cy] for v in q], ring_a)
            for c in range(phases):
                W2[c, b + 1, 0:cy] = W1[c, b + 1, 0:cy] + upper[c]
            if b in inner:
                lower = product(b, [v[cy:] for v in q], near_b)
                for c in range(phases):
                    W2[c, b + 1, cy : 2 * cy] = W1[c, b + 1, cy : 2 * cy] + lower[c]

        for b, applied in operate(lambda c, idx: W2[c, idx], inner):
            q = scaled(b, [H[c, b] - applied[c] for c in range(phases)])
            upper = product(b, [v[:cy] for v in q], ring_a)
            for c in range(phases):
                W1[c, b + 1, 0:cy] = W2[c, b + 1, 0:cy] + upper[c]

        for c in far:
            c.wait_recv()

        def weight(g, d):
            return CI[:, pl.ds(pl.multiple_of(g * tile, tile), tile)] * jnp.concatenate(
                [d] * (aggs // cy), axis=0)

        part = weight(me_w, XW[s])
        for d in range(1, nw):
            part = part + weight(lax.rem(me_w - d + nw, nw), GW[s, d - 1])
        sol = lax.dot_general(ones, part, NT, precision=HIGHEST, preferred_element_type=F32)
        ids = AG[...]
        lifted = jnp.zeros((rows_own, tile), F32)
        for g in range(aggs):
            value = jnp.broadcast_to(sol[0:1, g : g + 1], (rows_own, tile))
            lifted = jnp.where(ids == g, value, lifted)
        for c in range(phases):
            for p in range(px):
                new = CUR[s, c, p + 2, 0:cy] + W1[c, p + 2, 0:cy]
                if c == 0:
                    new = new + lifted[p * cy : (p + 1) * cy]
                CUR[s + 1, c, p + 2, 0:cy] = new
        for c in halo(s + 1):
            c.start()
        for c in near + far:
            c.wait_send()
        for c in halo(s):
            c.wait_send()
        return carry

    lax.fori_loop(0, SWEEPS, sweep, 0)
    for c in range(phases):
        out_it[c] = CUR[SWEEPS, c, 2 : 2 + px, 0:cy]
    for c in halo(SWEEPS):
        c.wait_recv()
    for b, applied in operate(lambda c, idx: CUR[SWEEPS, c, idx], inner):
        for c in range(phases):
            out_res[c, b - 1] = COEF[first_rhs + c, b + 1, 0:cy] - applied[c][:cy]
    for c in halo(SWEEPS) + coef:
        c.wait_send()


def solution(mesh):
    nw, nn = mesh.shape["wide"], mesh.shape["narrow"]

    def per_device(rhs, start, trans, accum, coupling, well_cells, well_index, agg_map, tile_factors, coarse_inverse):
        phases, px, cy, tile = rhs.shape
        box = px + 2
        aggs = coarse_inverse.shape[0]
        nch = 4 + phases * phases + phases
        vmem = pl.BlockSpec(memory_space=pltpu.VMEM)
        hbm = pl.BlockSpec(memory_space=pl.ANY)
        shape = jax.ShapeDtypeStruct(rhs.shape, F32)
        ring = (2 * cy, tile)
        dma = pltpu.SemaphoreType.DMA
        call = pl.pallas_call(
            functools.partial(body, nw, nn),
            out_shape=(shape, shape),
            in_specs=[hbm, hbm, hbm, hbm, hbm, vmem, vmem, hbm, hbm, hbm],
            out_specs=(vmem, vmem),
            scratch_shapes=[
                pltpu.VMEM((nch, px + 4) + ring, F32),
                pltpu.VMEM((SWEEPS + 1, phases, px + 4) + ring, F32),
                pltpu.VMEM((phases, px + 4) + ring, F32),
                pltpu.VMEM((phases, px + 4) + ring, F32),
                pltpu.VMEM((phases, box) + ring, F32),
                pltpu.VMEM((4 + 2 * phases, box) + ring, F32),
                pltpu.VMEM(tile_factors.shape, tile_factors.dtype),
                pltpu.VMEM(coarse_inverse.shape, F32),
                pltpu.VMEM((px * cy, tile), jnp.int32),
                pltpu.VMEM(accum.shape, F32),
                pltpu.VMEM((SWEEPS, nn - 1, cy, tile), F32),
                pltpu.VMEM((SWEEPS, nw - 1, cy, tile), F32),
                pltpu.VMEM((SWEEPS, cy, tile), F32),
                pltpu.VMEM((SWEEPS, cy, tile), F32),
                dma((8,)),
                dma((SWEEPS + 1, len(DIRS))),
                dma((SWEEPS + 1, len(DIRS))),
                dma((len(DIRS) + 3,)),
                dma((len(DIRS) + 3,)),
                dma((SWEEPS, nn - 1)),
                dma((SWEEPS, nn - 1)),
                dma((SWEEPS, nw - 1)),
                dma((SWEEPS, nw - 1)),
            ],
            compiler_params=pltpu.CompilerParams(collective_id=0, has_side_effects=True),
            name="schwarz",
        )
        return call(
            rhs, start, trans, accum,
            coupling.reshape((phases * phases,) + accum.shape),
            well_cells.reshape(1, -1), well_index.reshape(1, -1),
            agg_map.reshape(px * cy, tile), tile_factors, coarse_inverse)

    return jax.shard_map(
        per_device,
        mesh=mesh,
        in_specs=(
            P(None, "wide", "narrow", None),
            P(None, "wide", "narrow", None),
            P(None, "wide", "narrow", None),
            P("wide", "narrow", None),
            P(None, None, "wide", "narrow", None),
            P("wide", "narrow", None),
            P("wide", "narrow", None),
            P("wide", "narrow", None),
            P("wide", "narrow", None, None),
            P(("wide", "narrow"), None),
        ),
        out_specs=(P(None, "wide", "narrow", None), P(None, "wide", "narrow", None)),
        check_vma=False,
    )
```

time: 229 us -> 56.4 us (0.25); the launches traced: 226 us -> 56.1 us
  blocking collectives: 123 us -> 0 us
  Pallas kernels: 0 us -> 52.6 us
  starting transfers between devices: 34.2 us -> 0 us
  matrix products: 22.9 us -> 0 us
  waiting for transfers between devices: 18.4 us -> 0 us
  other arithmetic: 12.5 us -> 0 us
  local copies, waits for them, and re-layouts: 13.6 us -> 2.84 us
    unnamed x3 -> x0, blocking collectives: 123 us -> none
    pallas_call x0 -> x1, Pallas kernels: none -> 52.6 us  [per_device(): call(rhs, start, trans, accum, coupling.reshape((phases * phases,) + accu...]
    ppermute x20 -> x0, starting transfers between devices: 34.2 us -> none  [the longest x10 22.1 us: padded(): lax.ppermute(head, axis, [((i + 1) % count, i) for i in range(count)])]
    dot_general x18 -> x0, matrix products: 22.9 us -> none  [the longest x9 17 us: tile_apply(): jnp.einsum('cpyj,pykj->cpyk', scaled, factors, preferred_element_type=jnp...]
    ppermute x20 -> x0, waiting for transfers between devices: 18.4 us -> none  [the longest x10 16.2 us: padded(): lax.ppermute(tail, axis, [(i, (i + 1) % count) for i in range(count)])]
    slice x47 -> x0, local copies, waits for them, and re-layouts: 7.04 us -> none  [the longest x6 3.49 us: east_of(): return jnp.concatenate([values[..., middle:], from_next], axis=-1)]
    sub x3 -> x0, other arithmetic: 4.27 us -> none  [extended_fn(): extended = (rim_full[13:] - applied)[..., 1:-1, 1:-1, :]]
    reduce_sum x10 -> x0, other arithmetic: 2.64 us -> none  [operate(): mixing = jnp.sum(coupling * values[None], axis=1)]
  transfers between devices with their start and end apart: 20 -> 0, of which waited for: 13 -> 0; matrix products, arithmetic and copies ran while one was open for 1% -> 0% of each run, Pallas kernels for 0% -> 0%
where the time goes in v1:
time: 56.4 us; the launch traced here: 56.1 us
  Pallas kernels  52.6 us (93%)
  local copies, waits for them, and re-layouts  2.84 us (5%)
  between operations  0.64 us (1%)
    pallas_call x1, Pallas kernels, per_device(): call(rhs, start, trans, accum, coupling.reshape((phases * phases,) + accu...  52.6 us
    unnamed x2, local copies, waits for them, and re-layouts  2.84 us

profile of v1, /device:TPU:0, one launch (start us, length us, event | category | flops | bytes accessed | tf_op | source)
XLA Modules:
  0.0 56.1 jit_solution(5022384040759656899)
XLA Ops:
  0.6 52.6 %schwarz.1 = (f32[3,4,8,128]{3,2,1,0:T(8,128)}, f32[3,4,8,128]{3,2,1,0:T(8,128)}) custom-call(f32[3,4,8,128]{3,2,1,0:T(8,128)} %rhs.1, f32[3,4,8,128]{3,2,1,0:T(8,128)} %start.1, f32[3,4,8,128]{3,2,1,0:T(8,128)} %trans.1, f32[4,8,128]{2,1,0:T(8,128)} %accum.1, f32[9,4,8,128]{3,2,1,0:T(8,128)} %bitcast.4, s32[1,64]{1,0:T(1,128)} %bitcast.6, f32[1,64]{1,0:T(1,128)} %bitcast.7, ...), custom_call_target="tpu_custom_call" | custom-call | tf_op jit(solution)/shard_map/schwarz/pallas_call | solution.py:354
  53.3 1.4 %copy.14 = f32[3,4,8,128]{3,2,1,0:T(8,128)} copy(f32[3,4,8,128]{3,2,1,0:T(8,128)} %get-tuple-element.4) | data formatting | bytes 98304
  54.7 1.4 %copy.15 = f32[3,4,8,128]{3,2,1,0:T(8,128)} copy(f32[3,4,8,128]{3,2,1,0:T(8,128)} %get-tuple-element.5) | data formatting | bytes 98304

commit v2 on v1

--- a/solution.py
+++ b/solution.py
@@ -15,31 +15,29 @@
 DIRS = ((-1, 0), (1, 0), (0, -1), (0, 1), (-1, -1), (-1, 1), (1, -1), (1, 1))
 
 
-def halo_pieces(px, cy, depth_x, depth_y):
-    pieces = []
-    for dx, dy in DIRS:
-        if dx == 0:
-            sp, dp, np_ = 2, 2, px
-        elif dx > 0:
-            sp, dp, np_ = 2 + px - depth_x, 2 - depth_x, depth_x
-        else:
-            sp, dp, np_ = 2, 2 + px, depth_x
-        if dy == 0:
-            sr, dr, nr = 0, 0, cy
-        elif dy > 0:
-            sr, dr, nr = cy - depth_y, 2 * cy - depth_y, depth_y
-        else:
-            sr, dr, nr = 0, cy, depth_y
-        pieces.append(((sp, sr), (dp, dr), (np_, nr)))
-    return pieces
+def halo_piece(d, px, cy, depth_x, depth_y):
+    dx, dy = d
+    if dx == 0:
+        sp, dp, npair = 2, 2, px
+    elif dx > 0:
+        sp, dp, npair = 2 + px - depth_x, 2 - depth_x, depth_x
+    else:
+        sp, dp, npair = 2, 2 + px, depth_x
+    if dy == 0:
+        sr, dr, nrow = 0, 0, cy
+    elif dy > 0:
+        sr, dr, nrow = cy - depth_y, 2 * cy - depth_y, depth_y
+    else:
+        sr, dr, nrow = 0, cy, depth_y
+    return (pl.ds(sp, npair), pl.ds(sr, nrow)), (pl.ds(dp, npair), pl.ds(dr, nrow))
 
 
 def body(
     nw, nn,
     rhs, start, trans, accum, coupling, cells, widx, agg, tiles, cinv,
     out_it, out_res,
-    COEF, CUR, W1, W2, H, DER, TF, CI, AG, ACC, GN, GW, XN, XW,
-    loc, hs, hr, cs, cr, ns, nr, ws, wr,
+    COEF, CUR, FIX, W1, W2, H, DER, TF, CI, AG, AGX, ACC, GB, YB,
+    loc, hs, hr, cs, cr, gs, gr, is_, ir,
 ):
     phases = rhs.shape[0]
     px, cy, tile = accum.shape
@@ -70,8 +68,9 @@
         c.start()
 
     barrier = pltpu.get_barrier_semaphore()
-    peers = [(0, d) for d in range(1, nn)] + [(d, 0) for d in range(1, nw)]
-    peers += [d for d in DIRS if d[0] and d[1]]
+    peers = [(dw, dn) for dw in range(nw) for dn in range(nn) if dw or dn]
+    for p in range(px + 4):
+        AGX[p] = jnp.zeros((2 * cy, tile), jnp.int32)
     for d in peers:
         pl.semaphore_signal(barrier, inc=1, device_id=dev(*d), device_id_type=pl.DeviceIdType.MESH)
 
@@ -95,35 +94,40 @@
             device_id=dev(*d), device_id_type=pl.DeviceIdType.MESH,
         )
 
-    pieces = halo_pieces(px, cy, 2, 3)
-
     def halo(e):
         out = []
         for k, d in enumerate(DIRS):
-            (sp, sr), (dp, dr), (npair, nrow) = pieces[k]
-            out.append(remote(
-                CUR.at[e, :, pl.ds(sp, npair), pl.ds(sr, nrow)],
-                CUR.at[e, :, pl.ds(dp, npair), pl.ds(dr, nrow)],
-                hs.at[e, k], hr.at[e, k], d))
+            src, dst = halo_piece(d, px, cy, 2, 2 if d[0] else 3)
+            out.append(remote(CUR.at[(e, slice(None)) + src], CUR.at[(e, slice(None)) + dst],
+                              hs.at[e, k], hr.at[e, k], d))
         return out
 
     coef = []
+
+    def send_coef(channels, src, dst, d):
+        k = len(coef)
+        coef.append(remote(COEF.at[(channels,) + src], COEF.at[(channels,) + dst], cs.at[k], cr.at[k], d))
+
+    for d in DIRS:
+        depth_y = 1 if d[0] < 0 else 2
+        src, dst = halo_piece(d, px, cy, 1, depth_y)
+        send_coef(pl.ds(0, nch), src, dst, d)
+        if d[0] > 0:
+            (_, sr), (_, dr) = src, dst
+            send_coef(pl.ds(0, 1), (pl.ds(px, 1), sr), (pl.ds(0, 1), dr), d)
+        if d[1] > 0:
+            (sp, _), (dp, _) = src, dst
+            send_coef(pl.ds(1, 1), (sp, pl.ds(cy - depth_y - 1, 1)), (dp, pl.ds(2 * cy - depth_y - 1, 1)), d)
+
+    aggregates = []
     for k, d in enumerate(DIRS):
-        (sp, sr), (dp, dr), (npair, nrow) = halo_pieces(px, cy, 1, 3)[k]
-        coef.append(remote(
-            COEF.at[:, pl.ds(sp, npair), pl.ds(sr, nrow)],
-            COEF.at[:, pl.ds(dp, npair), pl.ds(dr, nrow)],
-            cs.at[k], cr.at[k], d))
-    extra = len(DIRS)
-    for k, d in enumerate(DIRS):
-        if d[0] > 0:
-            (sp, sr), (dp, dr), (npair, nrow) = pieces[k]
-            coef.append(remote(
-                COEF.at[pl.ds(0, 1), pl.ds(sp, 1), pl.ds(sr, nrow)],
-                COEF.at[pl.ds(0, 1), pl.ds(dp, 1), pl.ds(dr, nrow)],
-                cs.at[extra], cr.at[extra], d))
-            extra += 1
+        src, dst = halo_piece(d, px, cy, 2, 2 if d[0] else 3)
+        aggregates.append(remote(AGX.at[src], AGX.at[dst], is_.at[k], ir.at[k], d))
     for c in halo(0) + coef:
+        c.start()
+    local[5].wait()
+    AGX[2 : 2 + px, 0:cy] = (AG[...] + me_n * aggs).reshape(px, cy, tile)
+    for c in aggregates:
         c.start()
 
     lane = lax.broadcasted_iota(jnp.int32, (2 * cy, tile), 1)
@@ -137,7 +141,7 @@
             w[c, box + 1] = zero16
         W2[c, 1] = zero16
         W2[c, box] = zero16
-    for c in local[5:]:
+    for c in local[6:]:
         c.wait()
     for c in coef:
         c.wait_recv()
@@ -205,14 +209,15 @@
         return [DER[4 + phases + c, b] * h[c] for c in range(phases)]
 
     agg_iota = lax.broadcasted_iota(jnp.int32, (aggs, tile), 0)
-    lane8 = lax.broadcasted_iota(jnp.int32, (cy, tile), 1)
-    ones = jnp.ones((cy, tile), F32)
+
+    def current(e):
+        return lambda c, idx: FIX[idx] if c == 0 else CUR[e, c, idx]
 
     def sweep(s, carry):
-        for c in halo(s):
-            c.wait_recv()
+        read = current(s)
         acc = jnp.zeros((aggs, tile), F32)
-        for b, applied in operate(lambda c, idx: CUR[s, c, idx], range(box)):
+        order = list(inner) + [0, box - 1]
+        for b, applied in operate(read, order):
             h = [COEF[first_rhs + c, b + 1] - applied[c] for c in range(phases)]
             for c in range(phases):
                 H[c, b] = h[c]
@@ -220,11 +225,14 @@
                 for y in range(cy):
                     ids = AG[pl.ds((b - 1) * cy + y, 1), :]
                     acc = acc + jnp.where(agg_iota == ids, h[0][y : y + 1], 0.0)
-        wide_acc = jnp.concatenate([acc] * (tile // aggs), axis=0)
-        XN[s] = lax.dot_general(ones, wide_acc, NT, precision=HIGHEST, preferred_element_type=F32)
-        near = [remote(XN.at[s], GN.at[s, d - 1], ns.at[s, d - 1], nr.at[s, d - 1], (0, d))
-                for d in range(1, nn)]
-        for c in near:
+        sums = jnp.broadcast_to(jnp.sum(acc, axis=1, keepdims=True), (aggs, tile))
+        for g in range(nw):
+            y = jnp.sum(CI[:, g * tile : (g + 1) * tile] * sums, axis=0, keepdims=True)
+            for k in range(3):
+                YB[s, (g + 1 - k) % nw, k : k + 1] = y
+        share = [remote(YB.at[s, lax.rem(me_w + d[0], nw)], GB.at[s, k], gs.at[k], gr.at[s, k], d)
+                 for k, d in enumerate(peers)]
+        for c in share:
             c.start()
 
         for b in range(box):
@@ -234,18 +242,6 @@
             for c in range(phases):
                 W1[c, b + 1, 0:cy] = upper[c]
                 W1[c, b + 1, cy : 2 * cy] = lower[c]
-
-        for c in near:
-            c.wait_recv()
-        owner = lane8 // aggs
-        line = XN[s]
-        for d in range(1, nn):
-            line = jnp.where(owner == lax.rem(me_n - d + nn, nn), GN[s, d - 1], line)
-        XW[s] = line
-        far = [remote(XW.at[s], GW.at[s, d - 1], ws.at[s, d - 1], wr.at[s, d - 1], (d, 0))
-               for d in range(1, nw)]
-        for c in far:
-            c.start()
 
         for b, applied in operate(lambda c, idx: W1[c, idx], range(box)):
             q = scaled(b, [H[c, b] - applied[c] for c in range(phases)])
@@ -263,45 +259,42 @@
             for c in range(phases):
                 W1[c, b + 1, 0:cy] = W2[c, b + 1, 0:cy] + upper[c]
 
-        for c in far:
-            c.wait_recv()
-
-        def weight(g, d):
-            return CI[:, pl.ds(pl.multiple_of(g * tile, tile), tile)] * jnp.concatenate(
-                [d] * (aggs // cy), axis=0)
-
-        part = weight(me_w, XW[s])
-        for d in range(1, nw):
-            part = part + weight(lax.rem(me_w - d + nw, nw), GW[s, d - 1])
-        sol = lax.dot_general(ones, part, NT, precision=HIGHEST, preferred_element_type=F32)
-        ids = AG[...]
-        lifted = jnp.zeros((rows_own, tile), F32)
-        for g in range(aggs):
-            value = jnp.broadcast_to(sol[0:1, g : g + 1], (rows_own, tile))
-            lifted = jnp.where(ids == g, value, lifted)
         for c in range(phases):
             for p in range(px):
-                new = CUR[s, c, p + 2, 0:cy] + W1[c, p + 2, 0:cy]
-                if c == 0:
-                    new = new + lifted[p * cy : (p + 1) * cy]
-                CUR[s + 1, c, p + 2, 0:cy] = new
+                CUR[s + 1, c, p + 2, 0:cy] = read(c, p + 2)[:cy] + W1[c, p + 2, 0:cy]
         for c in halo(s + 1):
             c.start()
-        for c in near + far:
-            c.wait_send()
-        for c in halo(s):
+        for c in share:
+            c.wait_recv()
+        total = YB[s, me_w]
+        for k in range(len(peers)):
+            total = total + GB[s, k]
+        tables = [jnp.broadcast_to(total[k : k + 1], (2 * cy, tile)) for k in range(3)]
+        for c in halo(s + 1):
+            c.wait_recv()
+        for p in range(px + 4):
+            table = tables[0 if p < 2 else 1 if p < 2 + px else 2]
+            lifted = jnp.take_along_axis(table, AGX[p], axis=1, mode="promise_in_bounds")
+            FIX[p] = CUR[s + 1, 0, p] + lifted
+        for c in share + halo(s):
             c.wait_send()
         return carry
 
+    for c in halo(0):
+        c.wait_recv()
+    for p in range(px + 4):
+        FIX[p] = CUR[0, 0, p]
+    for c in aggregates:
+        c.wait_recv()
     lax.fori_loop(0, SWEEPS, sweep, 0)
+    last = current(SWEEPS)
     for c in range(phases):
-        out_it[c] = CUR[SWEEPS, c, 2 : 2 + px, 0:cy]
-    for c in halo(SWEEPS):
-        c.wait_recv()
-    for b, applied in operate(lambda c, idx: CUR[SWEEPS, c, idx], inner):
+        for p in range(px):
+            out_it[c, p] = last(c, p + 2)[:cy]
+    for b, applied in operate(last, inner):
         for c in range(phases):
             out_res[c, b - 1] = COEF[first_rhs + c, b + 1, 0:cy] - applied[c][:cy]
-    for c in halo(SWEEPS) + coef:
+    for c in halo(SWEEPS) + coef + aggregates:
         c.wait_send()
 
 
@@ -326,6 +319,7 @@
             scratch_shapes=[
                 pltpu.VMEM((nch, px + 4) + ring, F32),
                 pltpu.VMEM((SWEEPS + 1, phases, px + 4) + ring, F32),
+                pltpu.VMEM((px + 4,) + ring, F32),
                 pltpu.VMEM((phases, px + 4) + ring, F32),
                 pltpu.VMEM((phases, px + 4) + ring, F32),
                 pltpu.VMEM((phases, box) + ring, F32),
@@ -333,20 +327,19 @@
                 pltpu.VMEM(tile_factors.shape, tile_factors.dtype),
                 pltpu.VMEM(coarse_inverse.shape, F32),
                 pltpu.VMEM((px * cy, tile), jnp.int32),
+                pltpu.VMEM((px + 4,) + ring, jnp.int32),
                 pltpu.VMEM(accum.shape, F32),
-                pltpu.VMEM((SWEEPS, nn - 1, cy, tile), F32),
-                pltpu.VMEM((SWEEPS, nw - 1, cy, tile), F32),
-                pltpu.VMEM((SWEEPS, cy, tile), F32),
-                pltpu.VMEM((SWEEPS, cy, tile), F32),
+                pltpu.VMEM((SWEEPS, nw * nn - 1, 3, tile), F32),
+                pltpu.VMEM((SWEEPS, nw, 3, tile), F32),
                 dma((8,)),
                 dma((SWEEPS + 1, len(DIRS))),
                 dma((SWEEPS + 1, len(DIRS))),
-                dma((len(DIRS) + 3,)),
-                dma((len(DIRS) + 3,)),
-                dma((SWEEPS, nn - 1)),
-                dma((SWEEPS, nn - 1)),
-                dma((SWEEPS, nw - 1)),
-                dma((SWEEPS, nw - 1)),
+                dma((14,)),
+                dma((14,)),
+                dma((nw * nn - 1,)),
+                dma((SWEEPS, nw * nn - 1)),
+                dma((len(DIRS),)),
+                dma((len(DIRS),)),
             ],
             compiler_params=pltpu.CompilerParams(collective_id=0, has_side_effects=True),
             name="schwarz",

time: 56.4 us -> 41.9 us (0.74)
  Pallas kernels: 52.6 us -> 38.1 us
    pallas_call x1, Pallas kernels: 52.6 us -> 38.1 us  [per_device(): call(rhs, start, trans, accum, coupling.reshape((phases * phases,) + accu...]
where the time goes in v2:
time: 41.9 us; the launch traced here: 41.6 us
  Pallas kernels  38.1 us (91%)
  local copies, waits for them, and re-layouts  2.84 us (7%)
  between operations  0.64 us (2%)
    pallas_call x1, Pallas kernels, per_device(): call(rhs, start, trans, accum, coupling.reshape((phases * phases,) + accu...  38.1 us
    unnamed x2, local copies, waits for them, and re-layouts  2.84 us

profile of v2, /device:TPU:0, one launch (start us, length us, event | category | flops | bytes accessed | tf_op | source)
XLA Modules:
  0.0 41.6 jit_solution(10486105483612412396)
XLA Ops:
  0.6 38.1 %schwarz.1 = (f32[3,4,8,128]{3,2,1,0:T(8,128)}, f32[3,4,8,128]{3,2,1,0:T(8,128)}) custom-call(f32[3,4,8,128]{3,2,1,0:T(8,128)} %rhs.1, f32[3,4,8,128]{3,2,1,0:T(8,128)} %start.1, f32[3,4,8,128]{3,2,1,0:T(8,128)} %trans.1, f32[4,8,128]{2,1,0:T(8,128)} %accum.1, f32[9,4,8,128]{3,2,1,0:T(8,128)} %bitcast.4, s32[1,64]{1,0:T(1,128)} %bitcast.6, f32[1,64]{1,0:T(1,128)} %bitcast.7, ...), custom_call_target="tpu_custom_call" | custom-call | tf_op jit(solution)/shard_map/schwarz/pallas_call | solution.py:347
  38.8 1.4 %copy.14 = f32[3,4,8,128]{3,2,1,0:T(8,128)} copy(f32[3,4,8,128]{3,2,1,0:T(8,128)} %get-tuple-element.4) | data formatting | bytes 98304
  40.2 1.4 %copy.15 = f32[3,4,8,128]{3,2,1,0:T(8,128)} copy(f32[3,4,8,128]{3,2,1,0:T(8,128)} %get-tuple-element.5) | data formatting | bytes 98304

commit v3 on v2

--- a/solution.py
+++ b/solution.py
@@ -216,12 +216,11 @@
     def sweep(s, carry):
         read = current(s)
         acc = jnp.zeros((aggs, tile), F32)
-        order = list(inner) + [0, box - 1]
-        for b, applied in operate(read, order):
+        for b, applied in operate(read, inner):
             h = [COEF[first_rhs + c, b + 1] - applied[c] for c in range(phases)]
             for c in range(phases):
                 H[c, b] = h[c]
-            if b in inner:
+            if True:
                 for y in range(cy):
                     ids = AG[pl.ds((b - 1) * cy + y, 1), :]
                     acc = acc + jnp.where(agg_iota == ids, h[0][y : y + 1], 0.0)
@@ -234,6 +233,9 @@
                  for k, d in enumerate(peers)]
         for c in share:
             c.start()
+        for b, applied in operate(read, (0, box - 1)):
+            for c in range(phases):
+                H[c, b] = COEF[first_rhs + c, b + 1] - applied[c]
 
         for b in range(box):
             q = scaled(b, [H[c, b] for c in range(phases)])
@@ -296,6 +298,11 @@
             out_res[c, b - 1] = COEF[first_rhs + c, b + 1, 0:cy] - applied[c][:cy]
     for c in halo(SWEEPS) + coef + aggregates:
         c.wait_send()
+
+
+def hand_over(iterate, residual, out_it, out_res):
+    out_it[...] = iterate[...]
+    out_res[...] = residual[...]
 
 
 def solution(mesh):
@@ -344,11 +351,15 @@
             compiler_params=pltpu.CompilerParams(collective_id=0, has_side_effects=True),
             name="schwarz",
         )
-        return call(
+        held = call(
             rhs, start, trans, accum,
             coupling.reshape((phases * phases,) + accum.shape),
             well_cells.reshape(1, -1), well_index.reshape(1, -1),
             agg_map.reshape(px * cy, tile), tile_factors, coarse_inverse)
+        return pl.pallas_call(
+            hand_over, out_shape=(shape, shape), in_specs=[vmem, vmem], out_specs=(vmem, vmem),
+            name="hand_over",
+        )(*held)
 
     return jax.shard_map(
         per_device,

time: 41.9 us -> 40.4 us (0.964)
  local copies, waits for them, and re-layouts: 2.84 us -> 0 us
  Pallas kernels: 38.1 us -> 39.5 us
    unnamed x2 -> x0, local copies, waits for them, and re-layouts: 2.84 us -> none
    pallas_call x0 -> x1, Pallas kernels: none -> 1.46 us  [per_device(): pl.pallas_call(hand_over, out_shape=(shape, shape), in_specs=[vmem, vmem]...]
where the time goes in v3:
time: 40.4 us; the launch traced here: 40.1 us
  Pallas kernels  39.5 us (98%)
  between operations  0.64 us (2%)
    pallas_call x1, Pallas kernels, per_device(): call(rhs, start, trans, accum, coupling.reshape((phases * phases,) + accu...  38 us
    pallas_call x1, Pallas kernels, per_device(): pl.pallas_call(hand_over, out_shape=(shape, shape), in_specs=[vmem, vmem]...  1.46 us

profile of v3, /device:TPU:0, one launch (start us, length us, event | category | flops | bytes accessed | tf_op | source)
XLA Modules:
  0.0 40.1 jit_solution(14894893400179467076)
XLA Ops:
  0.6 38.0 %schwarz.1 = (f32[3,4,8,128]{3,2,1,0:T(8,128)}, f32[3,4,8,128]{3,2,1,0:T(8,128)}) custom-call(f32[3,4,8,128]{3,2,1,0:T(8,128)} %rhs.1, f32[3,4,8,128]{3,2,1,0:T(8,128)} %start.1, f32[3,4,8,128]{3,2,1,0:T(8,128)} %trans.1, f32[4,8,128]{2,1,0:T(8,128)} %accum.1, f32[9,4,8,128]{3,2,1,0:T(8,128)} %bitcast.4, s32[1,64]{1,0:T(1,128)} %bitcast.6, f32[1,64]{1,0:T(1,128)} %bitcast.7, ...), custom_call_target="tpu_custom_call" | custom-call | tf_op jit(solution)/shard_map/schwarz/pallas_call | solution.py:354
  38.7 1.5 %hand_over.1 = (f32[3,4,8,128]{3,2,1,0:T(8,128)}, f32[3,4,8,128]{3,2,1,0:T(8,128)}) custom-call(f32[3,4,8,128]{3,2,1,0:T(8,128)} %get-tuple-element.4.iterate, f32[3,4,8,128]{3,2,1,0:T(8,128)} %get-tuple-element.5.residual), custom_call_target="tpu_custom_call" | custom-call | tf_op jit(solution)/shard_map/hand_over/pallas_call | solution.py:359
